TPU v7x, 8 devices: a whole 2x2x1 slice. The times are simulated.
8 devices in a mesh: dp: 2 (over z, y), row: 2 (over x), fsdp: 2 (over core).
Axes of the slice: x: 2, y: 2, z: 1, core: 2. Of those that a mesh axis runs over, the one named last changes fastest.
Arguments:
- x_in: bfloat16 [32768, 768], P(('dp', 'row', 'fsdp'))
- dy_out: bfloat16 [32768, 768], P(('dp', 'row', 'fsdp'))
- w_gate: bfloat16 [768, 2048], P(None, ('row', 'fsdp'))
- w_up: bfloat16 [768, 2048], P(None, ('row', 'fsdp'))
- w_down: bfloat16 [2048, 768], P(('row', 'fsdp'))
- g_next: float32 [8, 3, 768, 2048], P(('dp', 'row', 'fsdp'))
Outputs:
- output 1: bfloat16 [32768, 768], P(('dp', 'row', 'fsdp'))
- output 2: float32 [3, 768, 2048], P(None, None, ('row', 'fsdp'))
- output 3: float32 [8, 3, 768, 2048], P(('dp', 'row', 'fsdp'))
All inputs are finite; a program needn't handle non-finite values.
Results may differ from a plain program's by a relative error of at most 0.0108919.
Values are sent between devices in bfloat16 or wider.
A program may use at most 1 GiB of HBM per device.

v0:
```python
import jax
import jax.numpy as jnp
from jax import lax
from jax.experimental import pallas as pl
from jax.experimental.pallas import tpu as pltpu
from jax.sharding import PartitionSpec as P

MESH = pl.DeviceIdType.MESH
GROUP_AXES = ("row", "fsdp")
ALL_AXES = ("dp", "row", "fsdp")
F32, BF16 = jnp.float32, jnp.bfloat16
CONTRACT_LAST = (((1,), (1,)), ((), ()))
CONTRACT_FIRST = (((0,), (0,)), ((), ()))
TOKENS, MODEL, HIDDEN = 4096, 768, 2048
HALF, SHARD = HIDDEN // 2, HIDDEN // 4
TILE = 512
STEPS = TOKENS // TILE
PIECES = 8
ROWS = 3 * MODEL // PIECES
SUB = ROWS // 2
VMEM_LIMIT = 63 * 2**20


def mm(lhs, rhs, dims=None):
    if dims is None:
        return jnp.dot(lhs, rhs, preferred_element_type=F32)
    return lax.dot_general(lhs, rhs, dims, preferred_element_type=F32)


def tile_backward(x, dy, w1, w3, w2, dw):
    a = mm(x, w1)
    b = mm(x, w3)
    dh = mm(dy, w2, CONTRACT_LAST)
    s = 0.5 * jnp.tanh(0.5 * a) + 0.5
    sa = a * s
    h = (sa * b).astype(BF16)
    da = (dh * b * (s + sa * (1.0 - s))).astype(BF16)
    db = (dh * sa).astype(BF16)
    dx = mm(da, w1, CONTRACT_LAST) + mm(db, w3, CONTRACT_LAST)
    dw[0] += mm(x, da, CONTRACT_FIRST)
    dw[1] += mm(x, db, CONTRACT_FIRST)
    dw[2] += mm(dy, h, CONTRACT_FIRST)
    return dx


def cols(index, width=SHARD):
    return pl.ds(pl.multiple_of(index * width, width), width)


def first_kernel(x_ref, dy_ref, s1, s3, s2, g, dx_ref, dwa_out, o1, o3, o2, q_keep, q_send,
                 w1, w3, w2, dw, gbuf, keep, send_a, recv_a, recv_b,
                 own_sem, wd_send, wd_recv, wx_send, wx_recv, wf_send, wf_recv,
                 g_sem, a_send, a_recv, b_send, b_recv, qk_sem, qs_sem, dw_sem):
    k = pl.program_id(0)
    dp, row, core = lax.axis_index("dp"), lax.axis_index("row"), lax.axis_index("fsdp")
    partner, x_next, y_next = (dp, row, 1 - core), (dp, 1 - row, core), (1 - dp, row, core)
    mine = cols(core)
    theirs = cols(1 - core)

    def remote(src, dst, send, recv, device):
        return pltpu.make_async_remote_copy(src_ref=src, dst_ref=dst, send_sem=send, recv_sem=recv, device_id=device, device_id_type=MESH)

    shards = (s1, s3, s2)
    near = (w1.at[:, mine], w3.at[:, mine], w2.at[mine, :])
    far = (o1.at[:, mine], o3.at[:, mine], o2.at[mine, :])
    own = [pltpu.make_async_copy(shards[i], near[i], own_sem.at[i]) for i in range(3)]
    to_partner = [remote(shards[i], near[i], wd_send.at[i], wd_recv.at[i], partner) for i in range(3)]
    to_x = [remote(shards[i], far[i], wx_send.at[i], wx_recv.at[i], x_next) for i in range(3)]
    forward = [remote(far[i], far[i], wf_send.at[i], wf_recv.at[i], partner) for i in range(3)]

    def load(i):
        return pltpu.make_async_copy(g.at[pl.ds(i * ROWS, ROWS), :], gbuf.at[i % 2], g_sem.at[i % 2])

    def to_a(i):
        return remote(send_a.at[i % 4], recv_a.at[i], a_send.at[i % 4], a_recv.at[i], partner)

    def to_b(i):
        part = keep.at[i, pl.ds(pl.multiple_of((1 - dp) * SUB, SUB), SUB), :]
        return remote(part, recv_b.at[i], b_send.at[i], b_recv.at[i], y_next)

    stay = pl.ds(pl.multiple_of(dp * SUB, SUB), SUB)

    def q_out(i):
        return (pltpu.make_async_copy(keep.at[i, stay, cols(row)], q_keep.at[i], qk_sem.at[i]),
                pltpu.make_async_copy(keep.at[i, stay, cols(1 - row)], q_send.at[i], qs_sem.at[i]))

    def cast(i):
        load(i).wait()
        for half in range(2):
            here = pl.ds(half * SHARD, SHARD)
            keep[i, :, here] = gbuf[i % 2, :, pl.ds(pl.multiple_of(half * HALF + core * SHARD, SHARD), SHARD)].astype(BF16)
            send_a[i % 4, :, here] = gbuf[i % 2, :, pl.ds(pl.multiple_of(half * HALF + (1 - core) * SHARD, SHARD), SHARD)].astype(BF16)
        to_a(i).start()

    def chip_sum(i):
        to_a(i).wait_recv()
        keep[i] = (keep[i].astype(F32) + recv_a[i].astype(F32)).astype(BF16)
        to_b(i).start()

    def pair_sum(i):
        to_b(i).wait_recv()
        keep[i, stay, :] = (keep[i, stay, :].astype(F32) + recv_b[i].astype(F32)).astype(BF16)
        for copy in q_out(i):
            copy.start()

    @pl.when(k == 0)
    def _():
        load(0).start()
        load(1).start()
        for copy in own:
            copy.start()
        barrier = pltpu.get_barrier_semaphore()
        for device in (partner, x_next, y_next):
            pl.semaphore_signal(barrier, inc=1, device_id=device, device_id_type=MESH)
        pl.semaphore_wait(barrier, 3)
        for copy in to_partner + to_x:
            copy.start()
        cast(0)
        load(2).start()
        cast(1)
        load(3).start()
        dw[...] = jnp.zeros_like(dw)
        chip_sum(0)
        for copy in own:
            copy.wait()
        for copy in to_partner:
            copy.wait_recv()

    @pl.when(k <= PIECES - 3)
    def _():
        @pl.when(k >= 2)
        def _():
            to_a(k - 2).wait_send()
        cast(k + 2)

        @pl.when(k <= PIECES - 5)
        def _():
            load(k + 4).start()

    @pl.when(k <= PIECES - 2)
    def _():
        chip_sum(k + 1)

    @pl.when(k >= 2)
    def _():
        pair_sum(k - 2)

    for at, i in ((2, 0), (5, 1), (7, 2)):
        @pl.when(k == at)
        def _():
            to_x[i].wait_recv()
            forward[i].start()

    dx_ref[...] = tile_backward(x_ref[...], dy_ref[...], w1[...], w3[...], w2[...], dw)

    @pl.when(k == STEPS - 1)
    def _():
        dw_copy = pltpu.make_async_copy(dw, dwa_out, dw_sem)
        dw_copy.start()
        pair_sum(PIECES - 2)
        pair_sum(PIECES - 1)
        for i in range(3):
            to_partner[i].wait_send()
            to_x[i].wait_send()
            forward[i].wait_send()
            forward[i].wait_recv()
        for i in range(PIECES - 4, PIECES):
            to_a(i).wait_send()
        for i in range(PIECES):
            to_b(i).wait_send()
            for copy in q_out(i):
                copy.wait()
        dw_copy.wait()


def second_kernel(x_ref, dy_ref, w1, w3, w2, dxp_ref, dwa_ref, dx_ref, dw_out, dw, pass_sem, dw_sem):
    k = pl.program_id(0)
    row = lax.axis_index("row")
    band = MODEL // STEPS
    passing = pltpu.make_async_copy(dwa_ref, dw_out.at[:, pl.ds(pl.multiple_of(k * band, band), band), cols(row, HALF)], pass_sem)
    passing.start()

    @pl.when(k == 0)
    def _():
        dw[...] = jnp.zeros_like(dw)

    dx = tile_backward(x_ref[...], dy_ref[...], w1[...], w3[...], w2[...], dw)
    dx_ref[...] = (dxp_ref[...] + dx).astype(BF16)
    passing.wait()

    @pl.when(k == STEPS - 1)
    def _():
        last = pltpu.make_async_copy(dw, dw_out.at[:, :, cols(1 - row, HALF)], dw_sem)
        last.start()
        last.wait()


def sum_kernel(keep_ref, x_ref, y_ref, d_ref, out_ref):
    dp = lax.axis_index("dp")
    here = pl.ds(pl.multiple_of(dp * SUB, SUB), SUB)
    there = pl.ds(pl.multiple_of((1 - dp) * SUB, SUB), SUB)
    out_ref[0, here, :] = keep_ref[0].astype(F32) + x_ref[0].astype(F32)
    out_ref[0, there, :] = y_ref[0].astype(F32) + d_ref[0].astype(F32)


def solution(mesh):
    any_spec = pl.BlockSpec(memory_space=pl.ANY)
    tile_spec = pl.BlockSpec((TILE, MODEL), lambda t: (t, 0))
    shape = jax.ShapeDtypeStruct
    dma = pltpu.SemaphoreType.DMA
    half_flops = 8 * 2 * TOKENS * MODEL * HALF

    def per_device(x_blk, dy_blk, gate, up, down, g_part):
        g2 = g_part.reshape(3 * MODEL, HIDDEN)
        dxp, dwa, o1, o3, o2, q_keep, q_send = pl.pallas_call(
            first_kernel,
            grid=(STEPS,),
            in_specs=[tile_spec, tile_spec] + [any_spec] * 4,
            out_specs=[tile_spec] + [any_spec] * 6,
            out_shape=[shape((TOKENS, MODEL), F32), shape((3, MODEL, HALF), F32), shape((MODEL, HALF), BF16), shape((MODEL, HALF), BF16),
                       shape((HALF, MODEL), BF16), shape((PIECES, SUB, SHARD), BF16), shape((PIECES, SUB, SHARD), BF16)],
            scratch_shapes=[
                pltpu.VMEM((MODEL, HALF), BF16), pltpu.VMEM((MODEL, HALF), BF16), pltpu.VMEM((HALF, MODEL), BF16),
                pltpu.VMEM((3, MODEL, HALF), F32), pltpu.VMEM((2, ROWS, HIDDEN), F32),
                pltpu.VMEM((PIECES, ROWS, HALF), BF16), pltpu.VMEM((4, ROWS, HALF), BF16), pltpu.VMEM((PIECES, ROWS, HALF), BF16),
                pltpu.VMEM((PIECES, SUB, HALF), BF16),
                dma((3,)), dma((3,)), dma((3,)), dma((3,)), dma((3,)), dma((3,)), dma((3,)),
                dma((2,)), dma((4,)), dma((PIECES,)), dma((PIECES,)), dma((PIECES,)), dma((PIECES,)), dma((PIECES,)), dma,
            ],
            compiler_params=pltpu.CompilerParams(vmem_limit_bytes=VMEM_LIMIT, collective_id=0, has_side_effects=True),
            cost_estimate=pl.CostEstimate(flops=half_flops, bytes_accessed=80 * 2**20, transcendentals=TOKENS * HALF),
            name="near_half",
        )(x_blk, dy_blk, gate, up, down, g2)

        devices = [(d, r, c) for d in range(2) for r in range(2) for c in range(2)]

        def number(d, r, c):
            return 4 * d + 2 * r + c

        from_x = lax.ppermute(q_send, ALL_AXES, [(number(d, r, c), number(d, 1 - r, c)) for d, r, c in devices])
        from_y = lax.ppermute(q_keep, ALL_AXES, [(number(d, r, c), number(1 - d, r, c)) for d, r, c in devices])
        from_diagonal = lax.ppermute(q_send, ALL_AXES, [(number(d, r, c), number(1 - d, 1 - r, c)) for d, r, c in devices])

        whole = pl.BlockSpec(memory_space=pltpu.VMEM)
        dx, dw_local = pl.pallas_call(
            second_kernel,
            grid=(STEPS,),
            in_specs=[tile_spec, tile_spec, whole, whole, whole, tile_spec, pl.BlockSpec((3, MODEL // STEPS, HALF), lambda t: (0, t, 0))],
            out_specs=[tile_spec, any_spec],
            out_shape=[shape((TOKENS, MODEL), BF16), shape((3, MODEL, HIDDEN), F32)],
            scratch_shapes=[pltpu.VMEM((3, MODEL, HALF), F32), dma, dma],
            compiler_params=pltpu.CompilerParams(vmem_limit_bytes=VMEM_LIMIT),
            cost_estimate=pl.CostEstimate(flops=half_flops, bytes_accessed=64 * 2**20, transcendentals=TOKENS * HALF),
            name="far_half",
        )(x_blk, dy_blk, o1, o3, o2, dxp, dwa)

        piece_spec = pl.BlockSpec((1, SUB, SHARD), lambda i: (i, 0, 0))
        dw_next = pl.pallas_call(
            sum_kernel,
            grid=(PIECES,),
            in_specs=[piece_spec] * 4,
            out_specs=pl.BlockSpec((1, ROWS, SHARD), lambda i: (i, 0, 0)),
            out_shape=shape((PIECES, ROWS, SHARD), F32),
            cost_estimate=pl.CostEstimate(flops=2**20, bytes_accessed=10 * 2**20, transcendentals=0),
            name="final_sum",
        )(q_keep, from_x, from_y, from_diagonal)
        return dx, dw_next.reshape(3, MODEL, SHARD), dw_local[None]

    return jax.shard_map(
        per_device,
        mesh=mesh,
        in_specs=(P(ALL_AXES, None), P(ALL_AXES, None), P(None, GROUP_AXES), P(None, GROUP_AXES), P(GROUP_AXES, None), P(ALL_AXES, None, None, None)),
        out_specs=(P(ALL_AXES, None), P(None, None, GROUP_AXES), P(ALL_AXES, None, None, None)),
        check_vma=False,
    )
```

profile of v0, /device:TPU:0, one launch (start us, length us, event | category | flops | bytes accessed | tf_op | source)
XLA Modules:
  0.0 147.2 jit_solution(15578318862418379884)
XLA Ops:
  0.6 72.6 %near_half.1 = (f32[4096,768]{1,0:T(8,128)}, f32[3,768,1024]{2,1,0:T(8,128)}, bf16[768,1024]{1,0:T(8,128)(2,1)}, bf16[768,1024]{1,0:T(8,128)(2,1)}, bf16[1024,76...) custom-call(bf16[4096,768]{1,0:T(8,128)(2,1)} %x_ref.3, bf16[4096,768]{1,0:T(8,128)(2,1)} %dy_ref.3, ...), custom_call_target="tpu_custom_call" | custom-call | flops 51539607552 | bytes 83886080 | tf_op jit(solution)/shard_map/near_half/pallas_call | solution.py:215
  73.2 1.8 %collective-permute-start.2 = (bf16[8,144,512]{2,1,0:T(8,128)(2,1)}, bf16[8,144,512]{2,1,0:T(8,128)(2,1)}, u32[]{:S(2)}, u32[]{:S(2)}) collective-permute-start(bf16[8,144,512]{2,1,0:T(8,128)(2,1)} %get-tuple-element.19), channel_id=1, source_target_pairs={{0,6},{1,7},{2,4},{3,5},{4,2},{5,3},{6,0},{7,1}} | collective-permute-start | bytes 3538952 | tf_op jit(solution)/shard_map/ppermute | solution.py:242
  75.0 1.1 collective-permute-start
  76.1 0.6 collective-permute-start.1
  76.7 63.5 %far_half.1 = (bf16[4096,768]{1,0:T(8,128)(2,1)}, f32[3,768,2048]{2,1,0:T(8,128)}) custom-call(bf16[4096,768]{1,0:T(8,128)(2,1)} %x_ref.3, bf16[4096,768]{1,0:T(8,128)(2,1)} %dy_ref.3, bf16[768,1024]{1,0:T(8,128)(2,1)} %get-tuple-element.12.w1, bf16[768,1024]{1,0:T(8,128)(2,1)} %get-tuple-element.13.w3, bf16[1024,768]{1,0:T(8,128)(2,1)} %get-tuple-element.14.w2, ...), custom_call_target="tpu_custom_call" | custom-call | flops 51539607552 | bytes 67108864 | tf_op jit(solution)/shard_map/far_half/pallas_call | solution.py:245
  140.2 0.0 collective-permute-done.1.y_ref
  140.3 0.0 collective-permute-done.2.d_ref
  140.3 0.0 collective-permute-done.x_ref
  140.3 6.9 %final_sum.1 = f32[8,288,512]{2,1,0:T(8,128)} custom-call(bf16[8,144,512]{2,1,0:T(8,128)(2,1)} %get-tuple-element.18.keep_ref, bf16[8,144,512]{2,1,0:T(8,128)(2,1)} %collective-permute-done.x_ref, bf16[8,144,512]{2,1,0:T(8,128)(2,1)} %collective-permute-done.1.y_ref, bf16[8,144,512]{2,1,0:T(8,128)(2,1)} %collective-permute-done.2.d_ref), custom_call_target="tpu_custom_call" | custom-call | flops 1048576 | bytes 10485760 | tf_op jit(solution)/shard_map/final_sum/pallas_call | solution.py:258
Async XLA Ops:
  73.2 67.1 %collective-permute-start.2 = (bf16[8,144,512]{2,1,0:T(8,128)(2,1)}, bf16[8,144,512]{2,1,0:T(8,128)(2,1)}, u32[]{:S(2)}, u32[]{:S(2)}) collective-permute-start(bf16[8,144,512]{2,1,0:T(8,128)(2,1)} %get-tuple-element.19), channel_id=1, source_target_pairs={{0,6},{1,7},{2,4},{3,5},{4,2},{5,3},{6,0},{7,1}} | collective-permute-start | bytes 3538952 | tf_op jit(solution)/shard_map/ppermute | solution.py:242
  75.0 65.3 %collective-permute-start = (bf16[8,144,512]{2,1,0:T(8,128)(2,1)}, bf16[8,144,512]{2,1,0:T(8,128)(2,1)}, u32[]{:S(2)}, u32[]{:S(2)}) collective-permute-start(bf16[8,144,512]{2,1,0:T(8,128)(2,1)} %get-tuple-element.19), channel_id=1, source_target_pairs={{0,2},{1,3},{2,0},{3,1},{4,6},{5,7},{6,4},{7,5}} | collective-permute-start | bytes 3538952 | tf_op jit(solution)/shard_map/ppermute | solution.py:240
  76.1 64.2 %collective-permute-start.1 = (bf16[8,144,512]{2,1,0:T(8,128)(2,1)}, bf16[8,144,512]{2,1,0:T(8,128)(2,1)}, u32[]{:S(2)}, u32[]{:S(2)}) collective-permute-start(bf16[8,144,512]{2,1,0:T(8,128)(2,1)} %get-tuple-element.18.keep_ref), channel_id=1, source_target_pairs={{0,4},{1,5},{2,6},{3,7},{4,0},{5,1},{6,2},{7,3}} | collective-permute-start | bytes 3538952 | tf_op jit(solution)/shard_map/ppermute | solution.py:241
where the time goes:
time: 147 us
  Pallas kernels  143 us (97%)
  starting transfers between devices  3.51 us (2%)
    pallas_call x1, Pallas kernels, per_device(): pl.pallas_call(first_kernel, grid=(STEPS,), in_specs=[tile_spec, tile_spe...  72.6 us
    pallas_call x1, Pallas kernels, per_device(): pl.pallas_call(second_kernel, grid=(STEPS,), in_specs=[tile_spec, tile_sp...  63.5 us
    pallas_call x1, Pallas kernels, per_device(): pl.pallas_call(sum_kernel, grid=(PIECES,), in_specs=[piece_spec] * 4, out...  6.95 us
  transfers between devices with their start and end apart: 3, of which 0 were waited for; matrix products, arithmetic and copies ran while one was open for 0% of the time, Pallas kernels for 43%

commit v1 on v0

--- a/solution.py
+++ b/solution.py
@@ -18,6 +18,7 @@
 PIECES = 8
 ROWS = 3 * MODEL // PIECES
 SUB = ROWS // 2
+GROUP = 2
 VMEM_LIMIT = 63 * 2**20
 
 
@@ -27,7 +28,7 @@
     return lax.dot_general(lhs, rhs, dims, preferred_element_type=F32)
 
 
-def tile_backward(x, dy, w1, w3, w2, dw):
+def tile_backward(x, dy, w1, w3, w2, dw, at=slice(None), first=False, flush=None):
     a = mm(x, w1)
     b = mm(x, w3)
     dh = mm(dy, w2, CONTRACT_LAST)
@@ -36,11 +37,12 @@
     h = (sa * b).astype(BF16)
     da = (dh * b * (s + sa * (1.0 - s))).astype(BF16)
     db = (dh * sa).astype(BF16)
-    dx = mm(da, w1, CONTRACT_LAST) + mm(db, w3, CONTRACT_LAST)
-    dw[0] += mm(x, da, CONTRACT_FIRST)
-    dw[1] += mm(x, db, CONTRACT_FIRST)
-    dw[2] += mm(dy, h, CONTRACT_FIRST)
-    return dx
+    for i, lhs, rhs in ((2, dy, h), (0, x, da), (1, x, db)):
+        grad = mm(lhs, rhs, CONTRACT_FIRST)
+        dw[i, :, at] = grad if first else dw[i, :, at] + grad
+        if flush is not None:
+            flush(i)
+    return mm(da, w1, CONTRACT_LAST) + mm(db, w3, CONTRACT_LAST)
 
 
 def cols(index, width=SHARD):
@@ -105,58 +107,64 @@
 
     @pl.when(k == 0)
     def _():
-        load(0).start()
-        load(1).start()
-        for copy in own:
-            copy.start()
         barrier = pltpu.get_barrier_semaphore()
         for device in (partner, x_next, y_next):
             pl.semaphore_signal(barrier, inc=1, device_id=device, device_id_type=MESH)
+        load(0).start()
+        for copy in own:
+            copy.start()
+        load(1).start()
         pl.semaphore_wait(barrier, 3)
-        for copy in to_partner + to_x:
+        for copy in to_x:
             copy.start()
         cast(0)
-        load(2).start()
-        cast(1)
-        load(3).start()
-        dw[...] = jnp.zeros_like(dw)
-        chip_sum(0)
+        for copy in to_partner:
+            copy.start()
         for copy in own:
             copy.wait()
+        dx_ref[...] = tile_backward(x_ref[...], dy_ref[...], w1[:, mine], w3[:, mine], w2[mine, :], dw, mine, first=True)
+        chip_sum(0)
+        cast(1)
+        load(2).start()
         for copy in to_partner:
             copy.wait_recv()
-
-    @pl.when(k <= PIECES - 3)
-    def _():
+        dx_ref[...] += tile_backward(x_ref[...], dy_ref[...], w1[:, theirs], w3[:, theirs], w2[theirs, :], dw, theirs, first=True)
+
+    @pl.when(k > 0)
+    def _():
+        chip_sum(k)
+
+        @pl.when(k <= PIECES - 2)
+        def _():
+            @pl.when(k >= 3)
+            def _():
+                to_a(k - 3).wait_send()
+            cast(k + 1)
+
+            @pl.when(k <= PIECES - 3)
+            def _():
+                load(k + 2).start()
+
         @pl.when(k >= 2)
         def _():
-            to_a(k - 2).wait_send()
-        cast(k + 2)
-
-        @pl.when(k <= PIECES - 5)
-        def _():
-            load(k + 4).start()
-
-    @pl.when(k <= PIECES - 2)
-    def _():
-        chip_sum(k + 1)
-
-    @pl.when(k >= 2)
-    def _():
-        pair_sum(k - 2)
-
-    for at, i in ((2, 0), (5, 1), (7, 2)):
-        @pl.when(k == at)
-        def _():
-            to_x[i].wait_recv()
-            forward[i].start()
-
-    dx_ref[...] = tile_backward(x_ref[...], dy_ref[...], w1[...], w3[...], w2[...], dw)
+            pair_sum(k - 2)
+
+        for at, i in ((3, 0), (6, 1)):
+            @pl.when(k == at)
+            def _():
+                to_x[i].wait_recv()
+                forward[i].start()
+
+    @pl.when(jnp.logical_and(k > 0, k < STEPS - 1))
+    def _():
+        dx_ref[...] = tile_backward(x_ref[...], dy_ref[...], w1[...], w3[...], w2[...], dw)
 
     @pl.when(k == STEPS - 1)
     def _():
-        dw_copy = pltpu.make_async_copy(dw, dwa_out, dw_sem)
-        dw_copy.start()
+        dw_out = [pltpu.make_async_copy(dw.at[i], dwa_out.at[i], dw_sem.at[i]) for i in range(3)]
+        dx_ref[...] = tile_backward(x_ref[...], dy_ref[...], w1[...], w3[...], w2[...], dw, flush=lambda i: dw_out[i].start())
+        to_x[2].wait_recv()
+        forward[2].start()
         pair_sum(PIECES - 2)
         pair_sum(PIECES - 1)
         for i in range(3):
@@ -170,7 +178,8 @@
             to_b(i).wait_send()
             for copy in q_out(i):
                 copy.wait()
-        dw_copy.wait()
+        for copy in dw_out:
+            copy.wait()
 
 
 def second_kernel(x_ref, dy_ref, w1, w3, w2, dxp_ref, dwa_ref, dx_ref, dw_out, dw, pass_sem, dw_sem):
@@ -184,23 +193,28 @@
     def _():
         dw[...] = jnp.zeros_like(dw)
 
-    dx = tile_backward(x_ref[...], dy_ref[...], w1[...], w3[...], w2[...], dw)
-    dx_ref[...] = (dxp_ref[...] + dx).astype(BF16)
+    @pl.when(k < STEPS - 1)
+    def _():
+        dx = tile_backward(x_ref[...], dy_ref[...], w1[...], w3[...], w2[...], dw)
+        dx_ref[...] = (dxp_ref[...] + dx).astype(BF16)
+
+    @pl.when(k == STEPS - 1)
+    def _():
+        last = [pltpu.make_async_copy(dw.at[i], dw_out.at[i, :, cols(1 - row, HALF)], dw_sem.at[i]) for i in range(3)]
+        dx = tile_backward(x_ref[...], dy_ref[...], w1[...], w3[...], w2[...], dw, flush=lambda i: last[i].start())
+        dx_ref[...] = (dxp_ref[...] + dx).astype(BF16)
+        for copy in last:
+            copy.wait()
+
     passing.wait()
-
-    @pl.when(k == STEPS - 1)
-    def _():
-        last = pltpu.make_async_copy(dw, dw_out.at[:, :, cols(1 - row, HALF)], dw_sem)
-        last.start()
-        last.wait()
 
 
 def sum_kernel(keep_ref, x_ref, y_ref, d_ref, out_ref):
     dp = lax.axis_index("dp")
     here = pl.ds(pl.multiple_of(dp * SUB, SUB), SUB)
     there = pl.ds(pl.multiple_of((1 - dp) * SUB, SUB), SUB)
-    out_ref[0, here, :] = keep_ref[0].astype(F32) + x_ref[0].astype(F32)
-    out_ref[0, there, :] = y_ref[0].astype(F32) + d_ref[0].astype(F32)
+    out_ref[:, here, :] = keep_ref[...].astype(F32) + x_ref[...].astype(F32)
+    out_ref[:, there, :] = y_ref[...].astype(F32) + d_ref[...].astype(F32)
 
 
 def solution(mesh):
@@ -225,7 +239,7 @@
                 pltpu.VMEM((PIECES, ROWS, HALF), BF16), pltpu.VMEM((4, ROWS, HALF), BF16), pltpu.VMEM((PIECES, ROWS, HALF), BF16),
                 pltpu.VMEM((PIECES, SUB, HALF), BF16),
                 dma((3,)), dma((3,)), dma((3,)), dma((3,)), dma((3,)), dma((3,)), dma((3,)),
-                dma((2,)), dma((4,)), dma((PIECES,)), dma((PIECES,)), dma((PIECES,)), dma((PIECES,)), dma((PIECES,)), dma,
+                dma((2,)), dma((4,)), dma((PIECES,)), dma((PIECES,)), dma((PIECES,)), dma((PIECES,)), dma((PIECES,)), dma((3,)),
             ],
             compiler_params=pltpu.CompilerParams(vmem_limit_bytes=VMEM_LIMIT, collective_id=0, has_side_effects=True),
             cost_estimate=pl.CostEstimate(flops=half_flops, bytes_accessed=80 * 2**20, transcendentals=TOKENS * HALF),
@@ -248,18 +262,18 @@
             in_specs=[tile_spec, tile_spec, whole, whole, whole, tile_spec, pl.BlockSpec((3, MODEL // STEPS, HALF), lambda t: (0, t, 0))],
             out_specs=[tile_spec, any_spec],
             out_shape=[shape((TOKENS, MODEL), BF16), shape((3, MODEL, HIDDEN), F32)],
-            scratch_shapes=[pltpu.VMEM((3, MODEL, HALF), F32), dma, dma],
+            scratch_shapes=[pltpu.VMEM((3, MODEL, HALF), F32), dma, dma((3,))],
             compiler_params=pltpu.CompilerParams(vmem_limit_bytes=VMEM_LIMIT),
             cost_estimate=pl.CostEstimate(flops=half_flops, bytes_accessed=64 * 2**20, transcendentals=TOKENS * HALF),
             name="far_half",
         )(x_blk, dy_blk, o1, o3, o2, dxp, dwa)
 
-        piece_spec = pl.BlockSpec((1, SUB, SHARD), lambda i: (i, 0, 0))
+        piece_spec = pl.BlockSpec((GROUP, SUB, SHARD), lambda i: (i, 0, 0))
         dw_next = pl.pallas_call(
             sum_kernel,
-            grid=(PIECES,),
+            grid=(PIECES // GROUP,),
             in_specs=[piece_spec] * 4,
-            out_specs=pl.BlockSpec((1, ROWS, SHARD), lambda i: (i, 0, 0)),
+            out_specs=pl.BlockSpec((GROUP, ROWS, SHARD), lambda i: (i, 0, 0)),
             out_shape=shape((PIECES, ROWS, SHARD), F32),
             cost_estimate=pl.CostEstimate(flops=2**20, bytes_accessed=10 * 2**20, transcendentals=0),
             name="final_sum",

time: 147 us -> 141 us (0.959)
  Pallas kernels: 143 us -> 136 us
    pallas_call x1, Pallas kernels: 72.6 us -> 69.9 us  [per_device(): pl.pallas_call(first_kernel, grid=(STEPS,), in_specs=[tile_spec, tile_spe...]
    pallas_call x1, Pallas kernels: 63.5 us -> 61.3 us  [per_device(): pl.pallas_call(second_kernel, grid=(STEPS,), in_specs=[tile_spec, tile_sp...]
    pallas_call x1, Pallas kernels: 6.95 us -> 5.03 us  [per_device(): pl.pallas_call(sum_kernel, grid=(PIECES // GROUP,), in_specs=[piece_spec]...]
  transfers between devices with their start and end apart: 3 -> 3, of which waited for: 0 -> 0; matrix products, arithmetic and copies ran while one was open for 0% -> 0% of each run, Pallas kernels for 43% -> 44%
where the time goes in v1:
time: 141 us; the launch traced here: 140 us
  Pallas kernels  136 us (96%)
  starting transfers between devices  3.51 us (2%)
    pallas_call x1, Pallas kernels, per_device(): pl.pallas_call(first_kernel, grid=(STEPS,), in_specs=[tile_spec, tile_spe...  69.9 us
    pallas_call x1, Pallas kernels, per_device(): pl.pallas_call(second_kernel, grid=(STEPS,), in_specs=[tile_spec, tile_sp...  61.3 us
    pallas_call x1, Pallas kernels, per_device(): pl.pallas_call(sum_kernel, grid=(PIECES // GROUP,), in_specs=[piece_spec]...  5.03 us
  transfers between devices with their start and end apart: 3, of which 0 were waited for; matrix products, arithmetic and copies ran while one was open for 0% of the time, Pallas kernels for 44%

profile of v1, /device:TPU:0, one launch (start us, length us, event | category | flops | bytes accessed | tf_op | source)
XLA Modules:
  0.0 140.4 jit_solution(13510884496157236826)
XLA Ops:
  0.6 69.9 %near_half.1 = (f32[4096,768]{1,0:T(8,128)}, f32[3,768,1024]{2,1,0:T(8,128)}, bf16[768,1024]{1,0:T(8,128)(2,1)}, bf16[768,1024]{1,0:T(8,128)(2,1)}, bf16[1024,76...) custom-call(bf16[4096,768]{1,0:T(8,128)(2,1)} %x_ref.3, bf16[4096,768]{1,0:T(8,128)(2,1)} %dy_ref.3, ...), custom_call_target="tpu_custom_call" | custom-call | flops 51539607552 | bytes 83886080 | tf_op jit(solution)/shard_map/near_half/pallas_call | solution.py:229
  70.5 2.2 %collective-permute-start.2 = (bf16[8,144,512]{2,1,0:T(8,128)(2,1)}, bf16[8,144,512]{2,1,0:T(8,128)(2,1)}, u32[]{:S(2)}, u32[]{:S(2)}) collective-permute-start(bf16[8,144,512]{2,1,0:T(8,128)(2,1)} %get-tuple-element.19), channel_id=1, source_target_pairs={{0,6},{1,7},{2,4},{3,5},{4,2},{5,3},{6,0},{7,1}} | collective-permute-start | bytes 3538952 | tf_op jit(solution)/shard_map/ppermute | solution.py:256
  72.7 0.5 collective-permute-start
  73.2 0.8 collective-permute-start.1
  74.0 61.3 %far_half.1 = (bf16[4096,768]{1,0:T(8,128)(2,1)}, f32[3,768,2048]{2,1,0:T(8,128)}) custom-call(bf16[4096,768]{1,0:T(8,128)(2,1)} %x_ref.3, bf16[4096,768]{1,0:T(8,128)(2,1)} %dy_ref.3, bf16[768,1024]{1,0:T(8,128)(2,1)} %get-tuple-element.12.w1, bf16[768,1024]{1,0:T(8,128)(2,1)} %get-tuple-element.13.w3, bf16[1024,768]{1,0:T(8,128)(2,1)} %get-tuple-element.14.w2, ...), custom_call_target="tpu_custom_call" | custom-call | flops 51539607552 | bytes 67108864 | tf_op jit(solution)/shard_map/far_half/pallas_call | solution.py:259
  135.3 0.0 collective-permute-done.1.y_ref
  135.4 0.0 collective-permute-done.2.d_ref
  135.4 0.0 collective-permute-done.x_ref
  135.4 5.0 %final_sum.1 = f32[8,288,512]{2,1,0:T(8,128)} custom-call(bf16[8,144,512]{2,1,0:T(8,128)(2,1)} %get-tuple-element.18.keep_ref, bf16[8,144,512]{2,1,0:T(8,128)(2,1)} %collective-permute-done.x_ref, bf16[8,144,512]{2,1,0:T(8,128)(2,1)} %collective-permute-done.1.y_ref, bf16[8,144,512]{2,1,0:T(8,128)(2,1)} %collective-permute-done.2.d_ref), custom_call_target="tpu_custom_call" | custom-call | flops 1048576 | bytes 10485760 | tf_op jit(solution)/shard_map/final_sum/pallas_call | solution.py:272
Async XLA Ops:
  70.5 64.8 %collective-permute-start.2 = (bf16[8,144,512]{2,1,0:T(8,128)(2,1)}, bf16[8,144,512]{2,1,0:T(8,128)(2,1)}, u32[]{:S(2)}, u32[]{:S(2)}) collective-permute-start(bf16[8,144,512]{2,1,0:T(8,128)(2,1)} %get-tuple-element.19), channel_id=1, source_target_pairs={{0,6},{1,7},{2,4},{3,5},{4,2},{5,3},{6,0},{7,1}} | collective-permute-start | bytes 3538952 | tf_op jit(solution)/shard_map/ppermute | solution.py:256
  72.7 62.7 %collective-permute-start = (bf16[8,144,512]{2,1,0:T(8,128)(2,1)}, bf16[8,144,512]{2,1,0:T(8,128)(2,1)}, u32[]{:S(2)}, u32[]{:S(2)}) collective-permute-start(bf16[8,144,512]{2,1,0:T(8,128)(2,1)} %get-tuple-element.19), channel_id=1, source_target_pairs={{0,2},{1,3},{2,0},{3,1},{4,6},{5,7},{6,4},{7,5}} | collective-permute-start | bytes 3538952 | tf_op jit(solution)/shard_map/ppermute | solution.py:254
  73.2 62.1 %collective-permute-start.1 = (bf16[8,144,512]{2,1,0:T(8,128)(2,1)}, bf16[8,144,512]{2,1,0:T(8,128)(2,1)}, u32[]{:S(2)}, u32[]{:S(2)}) collective-permute-start(bf16[8,144,512]{2,1,0:T(8,128)(2,1)} %get-tuple-element.18.keep_ref), channel_id=1, source_target_pairs={{0,4},{1,5},{2,6},{3,7},{4,0},{5,1},{6,2},{7,3}} | collective-permute-start | bytes 3538952 | tf_op jit(solution)/shard_map/ppermute | solution.py:255

commit v2 on v1

v2 whole, which is shorter than its diff:
```python
import jax
import jax.numpy as jnp
from jax import lax
from jax.experimental import pallas as pl
from jax.experimental.pallas import tpu as pltpu
from jax.sharding import PartitionSpec as P

MESH = pl.DeviceIdType.MESH
GROUP_AXES = ("row", "fsdp")
ALL_AXES = ("dp", "row", "fsdp")
F32, BF16 = jnp.float32, jnp.bfloat16
CONTRACT_LAST = (((1,), (1,)), ((), ()))
CONTRACT_FIRST = (((0,), (0,)), ((), ()))
TOKENS, MODEL, HIDDEN = 4096, 768, 2048
HALF, SHARD = HIDDEN // 2, HIDDEN // 4
TILE = 512
STEPS = TOKENS // TILE
PIECES = 8
ROWS = 3 * MODEL // PIECES
SUB = ROWS // 2
FAR = 4
VMEM_LIMIT = 63 * 2**20


def mm(lhs, rhs, dims=None):
    if dims is None:
        return jnp.dot(lhs, rhs, preferred_element_type=F32)
    return lax.dot_general(lhs, rhs, dims, preferred_element_type=F32)


def tile_backward(x, dy, w1, w3, w2, dw, at=slice(None), first=False, flush=None):
    a = mm(x, w1)
    b = mm(x, w3)
    dh = mm(dy, w2, CONTRACT_LAST)
    s = 0.5 * jnp.tanh(0.5 * a) + 0.5
    sa = a * s
    h = (sa * b).astype(BF16)
    da = (dh * b * (s + sa * (1.0 - s))).astype(BF16)
    db = (dh * sa).astype(BF16)
    for i, lhs, rhs in ((2, dy, h), (0, x, da), (1, x, db)):
        grad = mm(lhs, rhs, CONTRACT_FIRST)
        dw[i, :, at] = grad if first else dw[i, :, at] + grad
        if flush is not None:
            flush(i)
    return mm(da, w1, CONTRACT_LAST) + mm(db, w3, CONTRACT_LAST)


def cols(index, width=SHARD):
    return pl.ds(pl.multiple_of(index * width, width), width)


def first_kernel(x_ref, dy_ref, s1, s3, s2, g, dx_ref, dxp_out, dw_out, o1, o3, o2, fin_own, fin_other,
                 w1, w3, w2, dw, dxs, gbuf, keep, send_a, recv_a, recv_b, recv_c,
                 own_sem, wd_send, wd_recv, wx_send, wx_recv, wf_send, wf_recv, g_sem, a_send, a_recv, b_send, b_recv,
                 c_send, c_recv, f_send, f_recv, fin_sem, dw_sem, dx_sem, o_sem):
    k = pl.program_id(0)
    dp, row, core = lax.axis_index("dp"), lax.axis_index("row"), lax.axis_index("fsdp")
    partner, x_next, y_next = (dp, row, 1 - core), (dp, 1 - row, core), (1 - dp, row, core)
    mine = cols(core)
    theirs = cols(1 - core)
    half = k // STEPS
    slot = k % FAR

    def remote(src, dst, send, recv, device):
        return pltpu.make_async_remote_copy(src_ref=src, dst_ref=dst, send_sem=send, recv_sem=recv, device_id=device, device_id_type=MESH)

    shards = (s1, s3, s2)
    near = (w1.at[0, :, mine], w3.at[0, :, mine], w2.at[0, mine, :])
    far = (w1.at[1, :, mine], w3.at[1, :, mine], w2.at[1, mine, :])
    own = [pltpu.make_async_copy(shards[i], near[i], own_sem.at[i]) for i in range(3)]
    to_partner = [remote(shards[i], near[i], wd_send.at[i], wd_recv.at[i], partner) for i in range(3)]
    to_x = [remote(shards[i], far[i], wx_send.at[i], wx_recv.at[i], x_next) for i in range(3)]
    forward = [remote(far[i], far[i], wf_send.at[i], wf_recv.at[i], partner) for i in range(3)]
    far_out = [pltpu.make_async_copy(w.at[1], o, o_sem.at[i]) for i, (w, o) in enumerate(((w1, o1), (w3, o3), (w2, o2)))]

    def load(i):
        return pltpu.make_async_copy(g.at[pl.ds(i * ROWS, ROWS), :], gbuf.at[i % 2], g_sem.at[i % 2])

    def to_a(i):
        return remote(send_a.at[i % 4], recv_a.at[i], a_send.at[i % 4], a_recv.at[i], partner)

    def to_b(i):
        part = keep.at[i, pl.ds(pl.multiple_of((1 - dp) * SUB, SUB), SUB), :]
        return remote(part, recv_b.at[i], b_send.at[i], b_recv.at[i], y_next)

    stay = pl.ds(pl.multiple_of(dp * SUB, SUB), SUB)

    def to_c(i):
        return remote(keep.at[i, stay, cols(1 - row)], recv_c.at[i], c_send.at[i], c_recv.at[i], x_next)

    def to_f(i):
        return remote(keep.at[i, stay, cols(row)], fin_other.at[i], f_send.at[i], f_recv.at[i], y_next)

    def own_fin(i):
        return pltpu.make_async_copy(keep.at[i, stay, cols(row)], fin_own.at[i], fin_sem.at[i])

    def dx_out(i):
        return pltpu.make_async_copy(dxs.at[i], dxp_out.at[i], dx_sem.at[i])

    def cast(i):
        load(i).wait()
        for part in range(2):
            here = pl.ds(part * SHARD, SHARD)
            keep[i, :, here] = gbuf[i % 2, :, pl.ds(pl.multiple_of(part * HALF + core * SHARD, SHARD), SHARD)].astype(BF16)
            send_a[i % 4, :, here] = gbuf[i % 2, :, pl.ds(pl.multiple_of(part * HALF + (1 - core) * SHARD, SHARD), SHARD)].astype(BF16)
        to_a(i).start()

    def chip_sum(i):
        to_a(i).wait_recv()
        keep[i] = (keep[i].astype(F32) + recv_a[i].astype(F32)).astype(BF16)
        to_b(i).start()

    def pair_sum(i):
        to_b(i).wait_recv()
        keep[i, stay, :] = (keep[i, stay, :].astype(F32) + recv_b[i].astype(F32)).astype(BF16)
        to_c(i).start()

    def whole_sum(i):
        to_c(i).wait_recv()
        keep[i, stay, cols(row)] = (keep[i, stay, cols(row)].astype(F32) + recv_c[i].astype(F32)).astype(BF16)
        to_f(i).start()
        own_fin(i).start()

    @pl.when(k == 0)
    def _():
        barrier = pltpu.get_barrier_semaphore()
        for device in (partner, x_next, y_next):
            pl.semaphore_signal(barrier, inc=1, device_id=device, device_id_type=MESH)
        load(0).start()
        for copy in own:
            copy.start()
        load(1).start()
        pl.semaphore_wait(barrier, 3)
        for copy in to_x:
            copy.start()
        cast(0)
        for copy in to_partner:
            copy.start()
        for copy in own:
            copy.wait()
        dxs[0] = tile_backward(x_ref[...], dy_ref[...], w1[0, :, mine], w3[0, :, mine], w2[0, mine, :], dw, mine, first=True)
        chip_sum(0)
        cast(1)
        load(2).start()
        for copy in to_partner:
            copy.wait_recv()
        dxs[0] += tile_backward(x_ref[...], dy_ref[...], w1[0, :, theirs], w3[0, :, theirs], w2[0, theirs, :], dw, theirs, first=True)

    @pl.when(jnp.logical_and(k > 0, k < PIECES))
    def _():
        chip_sum(k)

        @pl.when(k <= PIECES - 2)
        def _():
            @pl.when(k >= 3)
            def _():
                to_a(k - 3).wait_send()
            cast(k + 1)

            @pl.when(k <= PIECES - 3)
            def _():
                load(k + 2).start()

        @pl.when(k <= FAR)
        def _():
            dx_out(k - 1).start()

        @pl.when(k >= FAR)
        def _():
            dx_out(k - FAR).wait()

        for at, i in ((3, 0), (5, 1), (7, 2)):
            @pl.when(k == at)
            def _():
                to_x[i].wait_recv()
                forward[i].start()

    @pl.when(jnp.logical_and(k >= 2, k <= PIECES + 1))
    def _():
        pair_sum(k - 2)

    @pl.when(k >= STEPS)
    def _():
        @pl.when(k == STEPS)
        def _():
            for i in range(3):
                forward[i].wait_recv()
                far_out[i].start()
            for i in range(3):
                pltpu.make_async_copy(dw.at[i], dw_out.at[0, i], dw_sem.at[i]).wait()
            dw[...] = jnp.zeros_like(dw)
        whole_sum(2 * (k - STEPS))
        whole_sum(2 * (k - STEPS) + 1)

    def finish(flush):
        dx = tile_backward(x_ref[...], dy_ref[...], w1[half], w3[half], w2[half], dw, flush=flush)
        total = dx + jnp.where(k >= STEPS, dxs[slot], 0.0)
        dxs[slot] = total
        dx_ref[...] = total.astype(BF16)

    ends = jnp.logical_or(k == STEPS - 1, k == STEPS + FAR - 1)

    @pl.when(jnp.logical_and(k > 0, jnp.logical_not(ends)))
    def _():
        finish(None)

    @pl.when(ends)
    def _():
        finish(lambda i: pltpu.make_async_copy(dw.at[i], dw_out.at[half, i], dw_sem.at[i]).start())

    @pl.when(k == STEPS + FAR - 1)
    def _():
        for i in range(3):
            to_partner[i].wait_send()
            to_x[i].wait_send()
            forward[i].wait_send()
            far_out[i].wait()
        for i in range(PIECES - 4, PIECES):
            to_a(i).wait_send()
        for i in range(PIECES):
            to_b(i).wait_send()
            to_c(i).wait_send()
            own_fin(i).wait()
            to_f(i).wait()
        for i in range(3):
            pltpu.make_async_copy(dw.at[i], dw_out.at[1, i], dw_sem.at[i]).wait()


def second_kernel(x_ref, dy_ref, w1, w3, w2, dxp_ref, dxq_ref, own_ref, other_ref, dw_part, dx_ref, next_ref, dw_out,
                  dw, near_buf, far_buf, near_in_sem, near_out_sem, far_in_sem, far_out_sem):
    k = pl.program_id(0)
    dp, row = lax.axis_index("dp"), lax.axis_index("row")
    near_in = [pltpu.make_async_copy(dw_part.at[0, i], near_buf.at[i], near_in_sem.at[i]) for i in range(3)]
    near_out = [pltpu.make_async_copy(near_buf.at[i], dw_out.at[i, :, cols(row, HALF)], near_out_sem.at[i]) for i in range(3)]
    far_in = [pltpu.make_async_copy(dw_part.at[1, i], far_buf.at[i], far_in_sem.at[i]) for i in range(3)]
    far_out = [pltpu.make_async_copy(dw.at[i], dw_out.at[i, :, cols(1 - row, HALF)], far_out_sem.at[i]) for i in range(3)]

    @pl.when(k == 0)
    def _():
        for copy in far_in + near_in:
            copy.start()
        dw[...] = jnp.zeros_like(dw)

    for i in range(3):
        @pl.when(k == i + 1)
        def _():
            far_in[i].wait()
            dw[i] += far_buf[i]
            near_in[i].wait()
            near_out[i].start()

    next_ref[:, pl.ds(pl.multiple_of(dp * SUB, SUB), SUB), :] = own_ref[...].astype(F32)
    next_ref[:, pl.ds(pl.multiple_of((1 - dp) * SUB, SUB), SUB), :] = other_ref[...].astype(F32)
    dx_ref[1] = dxq_ref[...]

    def finish(flush):
        dx = tile_backward(x_ref[...], dy_ref[...], w1[...], w3[...], w2[...], dw, flush=flush)
        dx_ref[0] = (dxp_ref[0] + dx).astype(BF16)

    @pl.when(k < FAR - 1)
    def _():
        finish(None)

    @pl.when(k == FAR - 1)
    def _():
        finish(lambda i: far_out[i].start())
        for copy in near_out + far_out:
            copy.wait()


def solution(mesh):
    any_spec = pl.BlockSpec(memory_space=pl.ANY)
    whole = pl.BlockSpec(memory_space=pltpu.VMEM)
    shape = jax.ShapeDtypeStruct
    dma = pltpu.SemaphoreType.DMA
    rest = STEPS - FAR
    tile_flops = 8 * 2 * TILE * MODEL * HALF

    def per_device(x_blk, dy_blk, gate, up, down, g_part):
        g2 = g_part.reshape(3 * MODEL, HIDDEN)
        spec = pl.BlockSpec((TILE, MODEL), lambda t: (jnp.where(t < STEPS, t, t - FAR), 0))
        dxq, dxp, dw_part, o1, o3, o2, fin_own, fin_other = pl.pallas_call(
            first_kernel,
            grid=(STEPS + FAR,),
            in_specs=[spec, spec] + [any_spec] * 4,
            out_specs=[pl.BlockSpec((TILE, MODEL), lambda t: (jnp.maximum(t - STEPS, 0), 0))] + [any_spec] * 7,
            out_shape=[shape((FAR * TILE, MODEL), BF16), shape((rest, TILE, MODEL), F32), shape((2, 3, MODEL, HALF), F32),
                       shape((MODEL, HALF), BF16), shape((MODEL, HALF), BF16), shape((HALF, MODEL), BF16),
                       shape((PIECES, SUB, SHARD), BF16), shape((PIECES, SUB, SHARD), BF16)],
            scratch_shapes=[
                pltpu.VMEM((2, MODEL, HALF), BF16), pltpu.VMEM((2, MODEL, HALF), BF16), pltpu.VMEM((2, HALF, MODEL), BF16),
                pltpu.VMEM((3, MODEL, HALF), F32), pltpu.VMEM((FAR, TILE, MODEL), F32), pltpu.VMEM((2, ROWS, HIDDEN), F32),
                pltpu.VMEM((PIECES, ROWS, HALF), BF16), pltpu.VMEM((4, ROWS, HALF), BF16), pltpu.VMEM((PIECES, ROWS, HALF), BF16),
                pltpu.VMEM((PIECES, SUB, HALF), BF16), pltpu.VMEM((PIECES, SUB, SHARD), BF16),
            ] + [dma((3,))] * 7 + [dma((2,)), dma((4,))] + [dma((PIECES,))] * 8 + [dma((3,)), dma((rest,)), dma((3,))],
            compiler_params=pltpu.CompilerParams(vmem_limit_bytes=VMEM_LIMIT, collective_id=0, has_side_effects=True),
            cost_estimate=pl.CostEstimate(flops=(STEPS + FAR) * tile_flops, bytes_accessed=100 * 2**20, transcendentals=TOKENS * HALF),
            name="near_and_far",
        )(x_blk, dy_blk, gate, up, down, g2)

        tile_spec = pl.BlockSpec((TILE, MODEL), lambda t: (t, 0))
        piece_spec = pl.BlockSpec((PIECES // rest, SUB, SHARD), lambda t: (t, 0, 0))
        dx, dw_next, dw_local = pl.pallas_call(
            second_kernel,
            grid=(rest,),
            in_specs=[tile_spec, tile_spec, whole, whole, whole, pl.BlockSpec((1, TILE, MODEL), lambda t: (t, 0, 0)), tile_spec, piece_spec, piece_spec, any_spec],
            out_specs=[pl.BlockSpec((2, TILE, MODEL), lambda t: (0, t, 0)), pl.BlockSpec((PIECES // rest, ROWS, SHARD), lambda t: (t, 0, 0)), any_spec],
            out_shape=[shape((2, TOKENS // 2, MODEL), BF16), shape((PIECES, ROWS, SHARD), F32), shape((3, MODEL, HIDDEN), F32)],
            scratch_shapes=[pltpu.VMEM((3, MODEL, HALF), F32)] * 3 + [dma((3,))] * 4,
            compiler_params=pltpu.CompilerParams(vmem_limit_bytes=VMEM_LIMIT),
            cost_estimate=pl.CostEstimate(flops=rest * tile_flops, bytes_accessed=70 * 2**20, transcendentals=TOKENS * HALF // 2),
            name="far_rest",
        )(x_blk, dy_blk, o1, o3, o2, dxp, dxq, fin_own, fin_other, dw_part)
        return dx.reshape(TOKENS, MODEL), dw_next.reshape(3, MODEL, SHARD), dw_local[None]

    return jax.shard_map(
        per_device,
        mesh=mesh,
        in_specs=(P(ALL_AXES, None), P(ALL_AXES, None), P(None, GROUP_AXES), P(None, GROUP_AXES), P(GROUP_AXES, None), P(ALL_AXES, None, None, None)),
        out_specs=(P(ALL_AXES, None), P(None, None, GROUP_AXES), P(ALL_AXES, None, None, None)),
        check_vma=False,
    )
```

time: 141 us -> 137 us (0.972)
  starting transfers between devices: 3.51 us -> 0 us
    ppermute x3 -> x0, starting transfers between devices: 3.51 us -> none  [the longest x1 2.19 us: per_device(): lax.ppermute(q_send, ALL_AXES, [(number(d, r, c), number(1 - d, 1 - r, c)...]
    pallas_call x3 -> x2, Pallas kernels: 136 us -> 136 us  [the longest x1 99.7 us: per_device(): pl.pallas_call(first_kernel, grid=(STEPS + FAR,), in_specs=[spec, spec] +...]
  transfers between devices with their start and end apart: 3 -> 0, of which waited for: 0 -> 0; matrix products, arithmetic and copies ran while one was open for 0% -> 0% of each run, Pallas kernels for 44% -> 0%
where the time goes in v2:
time: 137 us
  Pallas kernels  136 us (99%)
    pallas_call x1, Pallas kernels, per_device(): pl.pallas_call(first_kernel, grid=(STEPS + FAR,), in_specs=[spec, spec] +...  99.7 us
    pallas_call x1, Pallas kernels, per_device(): pl.pallas_call(second_kernel, grid=(rest,), in_specs=[tile_spec, tile_spe...  36.7 us

profile of v2, /device:TPU:0, one launch (start us, length us, event | category | flops | bytes accessed | tf_op | source)
XLA Modules:
  0.0 137.2 jit_solution(15348338874399911900)
XLA Ops:
  0.6 99.7 %near_and_far.1 = (bf16[2048,768]{1,0:T(8,128)(2,1)}, f32[4,512,768]{2,1,0:T(8,128)}, f32[2,3,768,1024]{3,2,1,0:T(8,128)}, bf16[768,1024]{1,0:T(8,128)(2,1)}, bf...) custom-call(bf16[4096,768]{1,0:T(8,128)(2,1)} %x_ref.3, ...), custom_call_target="tpu_custom_call" | custom-call | flops 77309411328 | bytes 104857600 | tf_op jit(solution)/shard_map/near_and_far/pallas_call | solution.py:282
  100.3 36.7 %far_rest.1 = (bf16[2,2048,768]{2,1,0:T(8,128)(2,1)}, f32[8,288,512]{2,1,0:T(8,128)}, f32[3,768,2048]{2,1,0:T(8,128)}) custom-call(bf16[4096,768]{1,0:T(8,128)(2,1)} %x_ref.3, bf16[4096,768]{1,0:T(8,128)(2,1)} %dy_ref.3, bf16[768,1024]{1,0:T(8,128)(2,1)} %get-tuple-element.14.w1, bf16[768,1024]{1,0:T(8,128)(2,1)} %get-tuple-element.15.w3, ...), custom_call_target="tpu_custom_call" | custom-call | flops 25769803776 | bytes 73400320 | tf_op jit(solution)/shard_map/far_rest/pallas_call | solution.py:303

commit v3 on v2

--- a/solution.py
+++ b/solution.py
@@ -49,10 +49,10 @@
     return pl.ds(pl.multiple_of(index * width, width), width)
 
 
-def first_kernel(x_ref, dy_ref, s1, s3, s2, g, dx_ref, dxp_out, dw_out, o1, o3, o2, fin_own, fin_other,
-                 w1, w3, w2, dw, dxs, gbuf, keep, send_a, recv_a, recv_b, recv_c,
+def first_kernel(x_hbm, dy_hbm, s1, s3, s2, g, dx_ref, dxp_out, dw_out, o1, o3, o2, fin_own, fin_other,
+                 w1, w3, w2, dw, dxs, gbuf, keep, send_a, recv_a, recv_b, recv_c, xs, dys,
                  own_sem, wd_send, wd_recv, wx_send, wx_recv, wf_send, wf_recv, g_sem, a_send, a_recv, b_send, b_recv,
-                 c_send, c_recv, f_send, f_recv, fin_sem, dw_sem, dx_sem, o_sem):
+                 c_send, c_recv, f_send, f_recv, fin_sem, dw_sem, dx_sem, o_sem, x_sem, dy_sem):
     k = pl.program_id(0)
     dp, row, core = lax.axis_index("dp"), lax.axis_index("row"), lax.axis_index("fsdp")
     partner, x_next, y_next = (dp, row, 1 - core), (dp, 1 - row, core), (1 - dp, row, core)
@@ -73,6 +73,11 @@
     forward = [remote(far[i], far[i], wf_send.at[i], wf_recv.at[i], partner) for i in range(3)]
     far_out = [pltpu.make_async_copy(w.at[1], o, o_sem.at[i]) for i, (w, o) in enumerate(((w1, o1), (w3, o3), (w2, o2)))]
 
+    def tokens(i):
+        rows = pl.ds(pl.multiple_of(jnp.where(i < STEPS, i, i - FAR) * TILE, TILE), TILE)
+        return (pltpu.make_async_copy(x_hbm.at[rows, :], xs.at[i % 2], x_sem.at[i % 2]),
+                pltpu.make_async_copy(dy_hbm.at[rows, :], dys.at[i % 2], dy_sem.at[i % 2]))
+
     def load(i):
         return pltpu.make_async_copy(g.at[pl.ds(i * ROWS, ROWS), :], gbuf.at[i % 2], g_sem.at[i % 2])
 
@@ -107,17 +112,17 @@
 
     def chip_sum(i):
         to_a(i).wait_recv()
-        keep[i] = (keep[i].astype(F32) + recv_a[i].astype(F32)).astype(BF16)
+        keep[i] = keep[i] + recv_a[i]
         to_b(i).start()
 
     def pair_sum(i):
         to_b(i).wait_recv()
-        keep[i, stay, :] = (keep[i, stay, :].astype(F32) + recv_b[i].astype(F32)).astype(BF16)
+        keep[i, stay, :] = keep[i, stay, :] + recv_b[i]
         to_c(i).start()
 
     def whole_sum(i):
         to_c(i).wait_recv()
-        keep[i, stay, cols(row)] = (keep[i, stay, cols(row)].astype(F32) + recv_c[i].astype(F32)).astype(BF16)
+        keep[i, stay, cols(row)] = keep[i, stay, cols(row)] + recv_c[i]
         to_f(i).start()
         own_fin(i).start()
 
@@ -126,25 +131,45 @@
         barrier = pltpu.get_barrier_semaphore()
         for device in (partner, x_next, y_next):
             pl.semaphore_signal(barrier, inc=1, device_id=device, device_id_type=MESH)
-        load(0).start()
+        for copy in tokens(0):
+            copy.start()
         for copy in own:
             copy.start()
-        load(1).start()
         pl.semaphore_wait(barrier, 3)
         for copy in to_x:
             copy.start()
+        for copy in tokens(0):
+            copy.wait()
+        for copy in own:
+            copy.wait()
+        for copy in to_partner:
+            copy.start()
+        load(0).start()
+        load(1).start()
+        for copy in tokens(1):
+            copy.start()
+        dxs[0] = tile_backward(xs[0], dys[0], w1[0, :, mine], w3[0, :, mine], w2[0, mine, :], dw, mine, first=True)
         cast(0)
-        for copy in to_partner:
-            copy.start()
-        for copy in own:
-            copy.wait()
-        dxs[0] = tile_backward(x_ref[...], dy_ref[...], w1[0, :, mine], w3[0, :, mine], w2[0, mine, :], dw, mine, first=True)
-        chip_sum(0)
+        load(2).start()
         cast(1)
-        load(2).start()
+        load(3).start()
         for copy in to_partner:
             copy.wait_recv()
-        dxs[0] += tile_backward(x_ref[...], dy_ref[...], w1[0, :, theirs], w3[0, :, theirs], w2[0, theirs, :], dw, theirs, first=True)
+        dxs[0] += tile_backward(xs[0], dys[0], w1[0, :, theirs], w3[0, :, theirs], w2[0, theirs, :], dw, theirs, first=True)
+
+    @pl.when(k > 0)
+    def _():
+        for copy in tokens(k):
+            copy.wait()
+
+        @pl.when(k < STEPS + FAR - 1)
+        def _():
+            for copy in tokens(k + 1):
+                copy.start()
+
+    @pl.when(k == 1)
+    def _():
+        chip_sum(0)
 
     @pl.when(jnp.logical_and(k > 0, k < PIECES))
     def _():
@@ -157,9 +182,9 @@
                 to_a(k - 3).wait_send()
             cast(k + 1)
 
-            @pl.when(k <= PIECES - 3)
+            @pl.when(k <= PIECES - 4)
             def _():
-                load(k + 2).start()
+                load(k + 3).start()
 
         @pl.when(k <= FAR)
         def _():
@@ -169,31 +194,38 @@
         def _():
             dx_out(k - FAR).wait()
 
-        for at, i in ((3, 0), (5, 1), (7, 2)):
+        for at, i in ((3, 0), (6, 1)):
             @pl.when(k == at)
             def _():
                 to_x[i].wait_recv()
                 forward[i].start()
 
-    @pl.when(jnp.logical_and(k >= 2, k <= PIECES + 1))
-    def _():
+    @pl.when(jnp.logical_and(k >= 3, k <= PIECES + 1))
+    def _():
+        @pl.when(k == 3)
+        def _():
+            pair_sum(0)
         pair_sum(k - 2)
 
     @pl.when(k >= STEPS)
     def _():
+        for at, pieces in enumerate(((0, 1), (2, 3), (4, 5, 6), (7,))):
+            @pl.when(k == STEPS + at)
+            def _():
+                for i in pieces:
+                    whole_sum(i)
+
         @pl.when(k == STEPS)
         def _():
+            for i in range(3):
+                pltpu.make_async_copy(dw.at[i], dw_out.at[0, i], dw_sem.at[i]).wait()
+            dw[...] = jnp.zeros_like(dw)
             for i in range(3):
                 forward[i].wait_recv()
                 far_out[i].start()
-            for i in range(3):
-                pltpu.make_async_copy(dw.at[i], dw_out.at[0, i], dw_sem.at[i]).wait()
-            dw[...] = jnp.zeros_like(dw)
-        whole_sum(2 * (k - STEPS))
-        whole_sum(2 * (k - STEPS) + 1)
 
     def finish(flush):
-        dx = tile_backward(x_ref[...], dy_ref[...], w1[half], w3[half], w2[half], dw, flush=flush)
+        dx = tile_backward(xs[k % 2], dys[k % 2], w1[half], w3[half], w2[half], dw, flush=flush)
         total = dx + jnp.where(k >= STEPS, dxs[slot], 0.0)
         dxs[slot] = total
         dx_ref[...] = total.astype(BF16)
@@ -207,6 +239,11 @@
     @pl.when(ends)
     def _():
         finish(lambda i: pltpu.make_async_copy(dw.at[i], dw_out.at[half, i], dw_sem.at[i]).start())
+
+    @pl.when(k == STEPS - 1)
+    def _():
+        to_x[2].wait_recv()
+        forward[2].start()
 
     @pl.when(k == STEPS + FAR - 1)
     def _():
@@ -226,20 +263,47 @@
             pltpu.make_async_copy(dw.at[i], dw_out.at[1, i], dw_sem.at[i]).wait()
 
 
-def second_kernel(x_ref, dy_ref, w1, w3, w2, dxp_ref, dxq_ref, own_ref, other_ref, dw_part, dx_ref, next_ref, dw_out,
-                  dw, near_buf, far_buf, near_in_sem, near_out_sem, far_in_sem, far_out_sem):
+def second_kernel(x_hbm, dy_hbm, o1, o3, o2, dxp, dxq, fin_own, fin_other, dw_part, dx_ref, next_ref, dw_out,
+                  w1, w3, w2, dw, near_buf, far_buf, xs, dys, dx_near, dx_done, own, other,
+                  in_sem, w_sem, near_in_sem, near_out_sem, far_in_sem, far_out_sem):
     k = pl.program_id(0)
     dp, row = lax.axis_index("dp"), lax.axis_index("row")
+    slot = k % 2
     near_in = [pltpu.make_async_copy(dw_part.at[0, i], near_buf.at[i], near_in_sem.at[i]) for i in range(3)]
     near_out = [pltpu.make_async_copy(near_buf.at[i], dw_out.at[i, :, cols(row, HALF)], near_out_sem.at[i]) for i in range(3)]
     far_in = [pltpu.make_async_copy(dw_part.at[1, i], far_buf.at[i], far_in_sem.at[i]) for i in range(3)]
     far_out = [pltpu.make_async_copy(dw.at[i], dw_out.at[i, :, cols(1 - row, HALF)], far_out_sem.at[i]) for i in range(3)]
+    weights = [pltpu.make_async_copy(o, w, w_sem.at[i]) for i, (o, w) in enumerate(((o1, w1), (o3, w3), (o2, w2)))]
+    group = PIECES // (STEPS - FAR)
+
+    def inputs(t):
+        rows = pl.ds(pl.multiple_of(t * TILE, TILE), TILE)
+        pieces = pl.ds(t * group, group)
+        pairs = ((x_hbm.at[rows, :], xs), (dy_hbm.at[rows, :], dys), (dxp.at[t], dx_near), (dxq.at[rows, :], dx_done),
+                 (fin_own.at[pieces], own), (fin_other.at[pieces], other))
+        return [pltpu.make_async_copy(src, dst.at[t % 2], in_sem.at[t % 2, i]) for i, (src, dst) in enumerate(pairs)]
 
     @pl.when(k == 0)
     def _():
-        for copy in far_in + near_in:
+        now = inputs(0)
+        for copy in now[:2] + weights + now[2:]:
             copy.start()
         dw[...] = jnp.zeros_like(dw)
+        for copy in weights:
+            copy.wait()
+
+    @pl.when(jnp.logical_and(k > 0, k < STEPS - FAR - 1))
+    def _():
+        for copy in inputs(k + 1):
+            copy.start()
+
+    for copy in inputs(k):
+        copy.wait()
+
+    @pl.when(k == 0)
+    def _():
+        for copy in inputs(1) + far_in + near_in:
+            copy.start()
 
     for i in range(3):
         @pl.when(k == i + 1)
@@ -249,19 +313,18 @@
             near_in[i].wait()
             near_out[i].start()
 
-    next_ref[:, pl.ds(pl.multiple_of(dp * SUB, SUB), SUB), :] = own_ref[...].astype(F32)
-    next_ref[:, pl.ds(pl.multiple_of((1 - dp) * SUB, SUB), SUB), :] = other_ref[...].astype(F32)
-    dx_ref[1] = dxq_ref[...]
-
     def finish(flush):
-        dx = tile_backward(x_ref[...], dy_ref[...], w1[...], w3[...], w2[...], dw, flush=flush)
-        dx_ref[0] = (dxp_ref[0] + dx).astype(BF16)
-
-    @pl.when(k < FAR - 1)
+        dx = tile_backward(xs[slot], dys[slot], w1[...], w3[...], w2[...], dw, flush=flush)
+        dx_ref[0] = (dx_near[slot] + dx).astype(BF16)
+        dx_ref[1] = dx_done[slot]
+        next_ref[:, pl.ds(pl.multiple_of(dp * SUB, SUB), SUB), :] = own[slot].astype(F32)
+        next_ref[:, pl.ds(pl.multiple_of((1 - dp) * SUB, SUB), SUB), :] = other[slot].astype(F32)
+
+    @pl.when(k < STEPS - FAR - 1)
     def _():
         finish(None)
 
-    @pl.when(k == FAR - 1)
+    @pl.when(k == STEPS - FAR - 1)
     def _():
         finish(lambda i: far_out[i].start())
         for copy in near_out + far_out:
@@ -270,7 +333,6 @@
 
 def solution(mesh):
     any_spec = pl.BlockSpec(memory_space=pl.ANY)
-    whole = pl.BlockSpec(memory_space=pltpu.VMEM)
     shape = jax.ShapeDtypeStruct
     dma = pltpu.SemaphoreType.DMA
     rest = STEPS - FAR
@@ -278,11 +340,10 @@
 
     def per_device(x_blk, dy_blk, gate, up, down, g_part):
         g2 = g_part.reshape(3 * MODEL, HIDDEN)
-        spec = pl.BlockSpec((TILE, MODEL), lambda t: (jnp.where(t < STEPS, t, t - FAR), 0))
         dxq, dxp, dw_part, o1, o3, o2, fin_own, fin_other = pl.pallas_call(
             first_kernel,
             grid=(STEPS + FAR,),
-            in_specs=[spec, spec] + [any_spec] * 4,
+            in_specs=[any_spec] * 6,
             out_specs=[pl.BlockSpec((TILE, MODEL), lambda t: (jnp.maximum(t - STEPS, 0), 0))] + [any_spec] * 7,
             out_shape=[shape((FAR * TILE, MODEL), BF16), shape((rest, TILE, MODEL), F32), shape((2, 3, MODEL, HALF), F32),
                        shape((MODEL, HALF), BF16), shape((MODEL, HALF), BF16), shape((HALF, MODEL), BF16),
@@ -292,21 +353,23 @@
                 pltpu.VMEM((3, MODEL, HALF), F32), pltpu.VMEM((FAR, TILE, MODEL), F32), pltpu.VMEM((2, ROWS, HIDDEN), F32),
                 pltpu.VMEM((PIECES, ROWS, HALF), BF16), pltpu.VMEM((4, ROWS, HALF), BF16), pltpu.VMEM((PIECES, ROWS, HALF), BF16),
                 pltpu.VMEM((PIECES, SUB, HALF), BF16), pltpu.VMEM((PIECES, SUB, SHARD), BF16),
-            ] + [dma((3,))] * 7 + [dma((2,)), dma((4,))] + [dma((PIECES,))] * 8 + [dma((3,)), dma((rest,)), dma((3,))],
+                pltpu.VMEM((2, TILE, MODEL), BF16), pltpu.VMEM((2, TILE, MODEL), BF16),
+            ] + [dma((3,))] * 7 + [dma((2,)), dma((4,))] + [dma((PIECES,))] * 8 + [dma((3,)), dma((rest,)), dma((3,)), dma((2,)), dma((2,))],
             compiler_params=pltpu.CompilerParams(vmem_limit_bytes=VMEM_LIMIT, collective_id=0, has_side_effects=True),
             cost_estimate=pl.CostEstimate(flops=(STEPS + FAR) * tile_flops, bytes_accessed=100 * 2**20, transcendentals=TOKENS * HALF),
             name="near_and_far",
         )(x_blk, dy_blk, gate, up, down, g2)
 
-        tile_spec = pl.BlockSpec((TILE, MODEL), lambda t: (t, 0))
-        piece_spec = pl.BlockSpec((PIECES // rest, SUB, SHARD), lambda t: (t, 0, 0))
         dx, dw_next, dw_local = pl.pallas_call(
             second_kernel,
             grid=(rest,),
-            in_specs=[tile_spec, tile_spec, whole, whole, whole, pl.BlockSpec((1, TILE, MODEL), lambda t: (t, 0, 0)), tile_spec, piece_spec, piece_spec, any_spec],
+            in_specs=[any_spec] * 10,
             out_specs=[pl.BlockSpec((2, TILE, MODEL), lambda t: (0, t, 0)), pl.BlockSpec((PIECES // rest, ROWS, SHARD), lambda t: (t, 0, 0)), any_spec],
             out_shape=[shape((2, TOKENS // 2, MODEL), BF16), shape((PIECES, ROWS, SHARD), F32), shape((3, MODEL, HIDDEN), F32)],
-            scratch_shapes=[pltpu.VMEM((3, MODEL, HALF), F32)] * 3 + [dma((3,))] * 4,
+            scratch_shapes=[pltpu.VMEM((MODEL, HALF), BF16), pltpu.VMEM((MODEL, HALF), BF16), pltpu.VMEM((HALF, MODEL), BF16)]
+            + [pltpu.VMEM((3, MODEL, HALF), F32)] * 3
+            + [pltpu.VMEM((2, TILE, MODEL), BF16), pltpu.VMEM((2, TILE, MODEL), BF16), pltpu.VMEM((2, TILE, MODEL), F32), pltpu.VMEM((2, TILE, MODEL), BF16)]
+            + [pltpu.VMEM((2, PIECES // rest, SUB, SHARD), BF16)] * 2 + [dma((2, 6))] + [dma((3,))] * 5,
             compiler_params=pltpu.CompilerParams(vmem_limit_bytes=VMEM_LIMIT),
             cost_estimate=pl.CostEstimate(flops=rest * tile_flops, bytes_accessed=70 * 2**20, transcendentals=TOKENS * HALF // 2),
             name="far_rest",

time: 137 us -> 133 us (0.971)
  Pallas kernels: 136 us -> 132 us
    pallas_call x2, Pallas kernels: 136 us -> 132 us  [the longest x1 96.6 us: per_device(): pl.pallas_call(first_kernel, grid=(STEPS + FAR,), in_specs=[any_spec] * 6...]
where the time goes in v3:
time: 133 us
  Pallas kernels  132 us (99%)
    pallas_call x1, Pallas kernels, per_device(): pl.pallas_call(first_kernel, grid=(STEPS + FAR,), in_specs=[any_spec] * 6...  96.6 us
    pallas_call x1, Pallas kernels, per_device(): pl.pallas_call(second_kernel, grid=(rest,), in_specs=[any_spec] * 10, out...  35.4 us

profile of v3, /device:TPU:0, one launch (start us, length us, event | category | flops | bytes accessed | tf_op | source)
XLA Modules:
  0.0 132.8 jit_solution(6334322151011347997)
XLA Ops:
  0.6 96.6 %near_and_far.1 = (bf16[2048,768]{1,0:T(8,128)(2,1)}, f32[4,512,768]{2,1,0:T(8,128)}, f32[2,3,768,1024]{3,2,1,0:T(8,128)}, bf16[768,1024]{1,0:T(8,128)(2,1)}, bf...) custom-call(bf16[4096,768]{1,0:T(8,128)(2,1)} %x_hbm.3, ...), custom_call_target="tpu_custom_call" | custom-call | flops 77309411328 | bytes 104857600 | tf_op jit(solution)/shard_map/near_and_far/pallas_call | solution.py:343
  97.2 35.4 %far_rest.1 = (bf16[2,2048,768]{2,1,0:T(8,128)(2,1)}, f32[8,288,512]{2,1,0:T(8,128)}, f32[3,768,2048]{2,1,0:T(8,128)}) custom-call(bf16[4096,768]{1,0:T(8,128)(2,1)} %x_hbm.3, bf16[4096,768]{1,0:T(8,128)(2,1)} %dy_hbm.3, bf16[768,1024]{1,0:T(8,128)(2,1)} %get-tuple-element.14.o1, bf16[768,1024]{1,0:T(8,128)(2,1)} %get-tuple-element.15.o3, ...), custom_call_target="tpu_custom_call" | custom-call | flops 25769803776 | bytes 73400320 | tf_op jit(solution)/shard_map/far_rest/pallas_call | solution.py:363

commit v4 on v3

--- a/solution.py
+++ b/solution.py
@@ -37,12 +37,16 @@
     h = (sa * b).astype(BF16)
     da = (dh * b * (s + sa * (1.0 - s))).astype(BF16)
     db = (dh * sa).astype(BF16)
+    if flush is None:
+        dx = mm(da, w1, CONTRACT_LAST) + mm(db, w3, CONTRACT_LAST)
     for i, lhs, rhs in ((2, dy, h), (0, x, da), (1, x, db)):
         grad = mm(lhs, rhs, CONTRACT_FIRST)
         dw[i, :, at] = grad if first else dw[i, :, at] + grad
         if flush is not None:
             flush(i)
-    return mm(da, w1, CONTRACT_LAST) + mm(db, w3, CONTRACT_LAST)
+    if flush is not None:
+        dx = mm(da, w1, CONTRACT_LAST) + mm(db, w3, CONTRACT_LAST)
+    return dx
 
 
 def cols(index, width=SHARD):

time: 133 us -> 133 us (level)
  no operation moved by 1% of the time
where the time goes in v4:
time: 133 us; the launch traced here: 132 us
  Pallas kernels  132 us (99%)
    pallas_call x1, Pallas kernels, per_device(): pl.pallas_call(first_kernel, grid=(STEPS + FAR,), in_specs=[any_spec] * 6...  96.4 us
    pallas_call x1, Pallas kernels, per_device(): pl.pallas_call(second_kernel, grid=(rest,), in_specs=[any_spec] * 10, out...  35.3 us

profile of v4, /device:TPU:0, one launch (start us, length us, event | category | flops | bytes accessed | tf_op | source)
XLA Modules:
  0.0 132.4 jit_solution(8275840563030494723)
XLA Ops:
  0.6 96.4 %near_and_far.1 = (bf16[2048,768]{1,0:T(8,128)(2,1)}, f32[4,512,768]{2,1,0:T(8,128)}, f32[2,3,768,1024]{3,2,1,0:T(8,128)}, bf16[768,1024]{1,0:T(8,128)(2,1)}, bf...) custom-call(bf16[4096,768]{1,0:T(8,128)(2,1)} %x_hbm.3, ...), custom_call_target="tpu_custom_call" | custom-call | flops 77309411328 | bytes 104857600 | tf_op jit(solution)/shard_map/near_and_far/pallas_call | solution.py:347
  97.0 35.3 %far_rest.1 = (bf16[2,2048,768]{2,1,0:T(8,128)(2,1)}, f32[8,288,512]{2,1,0:T(8,128)}, f32[3,768,2048]{2,1,0:T(8,128)}) custom-call(bf16[4096,768]{1,0:T(8,128)(2,1)} %x_hbm.3, bf16[4096,768]{1,0:T(8,128)(2,1)} %dy_hbm.3, bf16[768,1024]{1,0:T(8,128)(2,1)} %get-tuple-element.14.o1, bf16[768,1024]{1,0:T(8,128)(2,1)} %get-tuple-element.15.o3, ...), custom_call_target="tpu_custom_call" | custom-call | flops 25769803776 | bytes 73400320 | tf_op jit(solution)/shard_map/far_rest/pallas_call | solution.py:367
